TPU v7x, 8 devices: a whole 2x2x1 slice. The times are simulated.
8 devices in a mesh: parts: 1 (over z), data: 8 (over y, x, core).
Axes of the slice: x: 2, y: 2, z: 1, core: 2. Of those that a mesh axis runs over, the one named last changes fastest.
Arguments:
- feats: bfloat16 [8192, 784], P('data')
- labels: int32 [8192], P('data')
- w_in: float32 [784, 4, 800], P(None, 'parts')
- w_out: float32 [4, 800], P('parts')
- mom_in: float32 [784, 4, 800], P(None, 'parts')
- mom_out: float32 [4, 800], P('parts')
Outputs:
- output 1: float32 [784, 4, 800], P(None, 'parts')
- output 2: float32 [4, 800], P('parts')
- output 3: float32 [784, 4, 800], P(None, 'parts')
- output 4: float32 [4, 800], P('parts')
- output 5: float32 [4], P('parts')
All inputs are finite; a program needn't handle non-finite values.
Results may differ from a plain program's by a relative error of at most 0.001.
Values are sent between devices in bfloat16 or wider.
A program may use at most 1 GiB of HBM per device.

v0:
```python
import math
import jax
import jax.numpy as jnp
from jax import lax
from jax.sharding import PartitionSpec as P

LEAPS = 16
PRIOR_VAR = 1.0


def local_terms(x_rows, lab_rows, w_flat, pos_out):
    num_chain, hidden = pos_out.shape
    num_rows = x_rows.shape[0]
    pre_act = jnp.dot(x_rows, w_flat, preferred_element_type=jnp.float32).reshape(num_rows, num_chain, hidden)
    hidden_act = jnp.tanh(pre_act)
    logits = jnp.sum(hidden_act * pos_out, axis=-1)
    residual = lab_rows[:, None] - jax.nn.sigmoid(logits)
    grad_out = jnp.sum(hidden_act * residual[:, :, None], axis=0)
    back_grad = (residual[:, :, None] * pos_out * (1.0 - hidden_act * hidden_act)).astype(jnp.bfloat16)
    grad_in = lax.dot_general(x_rows, back_grad.reshape(num_rows, num_chain * hidden), (((0,), (0,)), ((), ())), preferred_element_type=jnp.float32)
    return grad_in.reshape(w_flat.shape[0], num_chain, hidden), grad_out, logits


def solution(mesh):
    row_spec = P('data', None)
    label_spec = P('data')
    in_spec = P(None, 'parts', None)
    out_spec = P('parts', None)
    chain_spec = P('parts')

    def run_chains(feats, labels, w_in, w_out, mom_in, mom_out):
        num_rows, num_feat = feats.shape
        hidden = w_in.shape[2]
        step_size = 1.0 / math.sqrt(num_rows * (num_feat + hidden))
        half_step = 0.5 * step_size

        def device_body(x_rows, y_rows, pos_in, pos_out, vel_in, vel_out):
            lab_rows = y_rows.astype(jnp.float32)
            num_chain = pos_out.shape[0]

            def log_post_grad(pos_in, pos_out):
                w_flat = pos_in.astype(jnp.bfloat16).reshape(num_feat, num_chain * hidden)
                grad_in, grad_out, logits = local_terms(x_rows, lab_rows, w_flat, pos_out)
                grad_in, grad_out = lax.psum((grad_in, grad_out), 'data')
                return grad_in - pos_in / PRIOR_VAR, grad_out - pos_out / PRIOR_VAR, logits

            def leap_step(step_index, state_now):
                pos_in, pos_out, vel_in, vel_out = state_now
                pos_in = pos_in + step_size * vel_in
                pos_out = pos_out + step_size * vel_out
                grad_in, grad_out, logits = log_post_grad(pos_in, pos_out)
                return pos_in, pos_out, vel_in + step_size * grad_in, vel_out + step_size * grad_out

            grad_in, grad_out, logits = log_post_grad(pos_in, pos_out)
            vel_in = vel_in + half_step * grad_in
            vel_out = vel_out + half_step * grad_out
            pos_in, pos_out, vel_in, vel_out = lax.fori_loop(0, LEAPS - 1, leap_step, (pos_in, pos_out, vel_in, vel_out))
            pos_in = pos_in + step_size * vel_in
            pos_out = pos_out + step_size * vel_out
            grad_in, grad_out, logits = log_post_grad(pos_in, pos_out)
            vel_in = vel_in + half_step * grad_in
            vel_out = vel_out + half_step * grad_out
            row_loss = jnp.sum(jax.nn.softplus(logits) - lab_rows[:, None] * logits, axis=0)
            row_loss = lax.psum(row_loss, 'data')
            energy = row_loss + (jnp.sum(pos_in * pos_in, axis=(0, 2)) + jnp.sum(pos_out * pos_out, axis=1)) / (2.0 * PRIOR_VAR) + 0.5 * (jnp.sum(vel_in * vel_in, axis=(0, 2)) + jnp.sum(vel_out * vel_out, axis=1))
            return pos_in, pos_out, vel_in, vel_out, energy

        mapped = jax.shard_map(device_body, mesh=mesh, in_specs=(row_spec, label_spec, in_spec, out_spec, in_spec, out_spec), out_specs=(in_spec, out_spec, in_spec, out_spec, chain_spec), check_vma=False)
        return mapped(feats, labels, w_in, w_out, mom_in, mom_out)

    return run_chains
```

profile of v0, /device:TPU:0, one launch (start us, length us, event | category | flops | bytes accessed | tf_op | source)
XLA Modules:
  0.0 4124.5 jit_solution(1681635464233780903)
XLA Ops:
  86.2 26.0 psum.50
  112.2 124.2 %all-reduce.5.cloned.1.call-done = f32[784,4,800]{2,1,0:T(4,128)} async-done(((f32[784,4,800]{2,1,0:T(4,128)}), f32[784,4,800]{2,1,0:T(4,128)}) %all-reduce.5.cloned.1.call-update) | async-done | bytes 10035216 | tf_op jit(solution)/shard_map/psum | solution.py:44
  236.4 16.2 multiply_add_fusion.6
  252.6 3616.4 %while.16 = (s32[]{:T(128)}, f32[784,4,800]{2,1,0:T(4,128)}, f32[4,800]{1,0:T(4,128)S(1)}, f32[784,4,800]{2,1,0:T(4,128)}, f32[4,800]{1,0:T(4,128)S(1)}, /*index...) while((s32[]{:T(128)}, f32[784,4,800]{2,1,0:T(4,128)}, f32[4,800]{1,0:T(4,128)S(1)}, ...), condition=%wide.region_9.0_spmd, body=%wide.region_4.0_spmd.sunk | while | flops 10323126272 | bytes 291418336 | solution.py:57
  265.0 15.4 fusion.34
  341.6 23.1 psum.57
  364.8 124.2 %all-reduce.9.cloned.1.call-done = f32[784,4,800]{2,1,0:T(4,128)} async-done(((f32[784,4,800]{2,1,0:T(4,128)}), f32[784,4,800]{2,1,0:T(4,128)}) %all-reduce.9.cloned.1.call-update) | async-done | bytes 10035216 | tf_op jit(solution)/shard_map/while/body/eval_jaxpr/psum | solution.py:44
  488.9 16.2 multiply_add_fusion.20
  505.3 15.4 fusion.34
  581.9 23.1 psum.57
  605.0 124.2 %all-reduce.9.cloned.1.call-done = f32[784,4,800]{2,1,0:T(4,128)} async-done(((f32[784,4,800]{2,1,0:T(4,128)}), f32[784,4,800]{2,1,0:T(4,128)}) %all-reduce.9.cloned.1.call-update) | async-done | bytes 10035216 | tf_op jit(solution)/shard_map/while/body/eval_jaxpr/psum | solution.py:44
  729.2 16.2 multiply_add_fusion.20
  745.5 15.4 fusion.34
  822.1 23.1 psum.57
  845.3 124.2 %all-reduce.9.cloned.1.call-done = f32[784,4,800]{2,1,0:T(4,128)} async-done(((f32[784,4,800]{2,1,0:T(4,128)}), f32[784,4,800]{2,1,0:T(4,128)}) %all-reduce.9.cloned.1.call-update) | async-done | bytes 10035216 | tf_op jit(solution)/shard_map/while/body/eval_jaxpr/psum | solution.py:44
  969.4 16.2 multiply_add_fusion.20
  1062.4 23.1 psum.57
  1085.5 124.2 %all-reduce.9.cloned.1.call-done = f32[784,4,800]{2,1,0:T(4,128)} async-done(((f32[784,4,800]{2,1,0:T(4,128)}), f32[784,4,800]{2,1,0:T(4,128)}) %all-reduce.9.cloned.1.call-update) | async-done | bytes 10035216 | tf_op jit(solution)/shard_map/while/body/eval_jaxpr/psum | solution.py:44
  1209.7 16.2 multiply_add_fusion.20
  1226.0 15.4 fusion.34
  1302.6 23.1 psum.57
  1325.8 124.2 %all-reduce.9.cloned.1.call-done = f32[784,4,800]{2,1,0:T(4,128)} async-done(((f32[784,4,800]{2,1,0:T(4,128)}), f32[784,4,800]{2,1,0:T(4,128)}) %all-reduce.9.cloned.1.call-update) | async-done | bytes 10035216 | tf_op jit(solution)/shard_map/while/body/eval_jaxpr/psum | solution.py:44
  1449.9 16.2 multiply_add_fusion.20
  1542.9 23.1 psum.57
  1566.0 124.2 %all-reduce.9.cloned.1.call-done = f32[784,4,800]{2,1,0:T(4,128)} async-done(((f32[784,4,800]{2,1,0:T(4,128)}), f32[784,4,800]{2,1,0:T(4,128)}) %all-reduce.9.cloned.1.call-update) | async-done | bytes 10035216 | tf_op jit(solution)/shard_map/while/body/eval_jaxpr/psum | solution.py:44
  1690.2 16.2 multiply_add_fusion.20
  1706.5 15.4 fusion.34
  1783.1 23.1 psum.57
  1806.3 124.2 %all-reduce.9.cloned.1.call-done = f32[784,4,800]{2,1,0:T(4,128)} async-done(((f32[784,4,800]{2,1,0:T(4,128)}), f32[784,4,800]{2,1,0:T(4,128)}) %all-reduce.9.cloned.1.call-update) | async-done | bytes 10035216 | tf_op jit(solution)/shard_map/while/body/eval_jaxpr/psum | solution.py:44
  1930.4 16.2 multiply_add_fusion.20
  1946.8 15.4 fusion.34
  2023.4 23.1 psum.57
  2046.5 124.2 %all-reduce.9.cloned.1.call-done = f32[784,4,800]{2,1,0:T(4,128)} async-done(((f32[784,4,800]{2,1,0:T(4,128)}), f32[784,4,800]{2,1,0:T(4,128)}) %all-reduce.9.cloned.1.call-update) | async-done | bytes 10035216 | tf_op jit(solution)/shard_map/while/body/eval_jaxpr/psum | solution.py:44
  2170.7 16.2 multiply_add_fusion.20
  2187.0 15.4 fusion.34
  2263.6 23.1 psum.57
  2286.7 124.2 %all-reduce.9.cloned.1.call-done = f32[784,4,800]{2,1,0:T(4,128)} async-done(((f32[784,4,800]{2,1,0:T(4,128)}), f32[784,4,800]{2,1,0:T(4,128)}) %all-reduce.9.cloned.1.call-update) | async-done | bytes 10035216 | tf_op jit(solution)/shard_map/while/body/eval_jaxpr/psum | solution.py:44
  2410.9 16.2 multiply_add_fusion.20
  2427.3 15.4 fusion.34
  2503.9 23.1 psum.57
  2527.0 124.2 %all-reduce.9.cloned.1.call-done = f32[784,4,800]{2,1,0:T(4,128)} async-done(((f32[784,4,800]{2,1,0:T(4,128)}), f32[784,4,800]{2,1,0:T(4,128)}) %all-reduce.9.cloned.1.call-update) | async-done | bytes 10035216 | tf_op jit(solution)/shard_map/while/body/eval_jaxpr/psum | solution.py:44
  2651.2 16.2 multiply_add_fusion.20
  2667.5 15.4 fusion.34
  2744.1 23.1 psum.57
  2767.2 124.2 %all-reduce.9.cloned.1.call-done = f32[784,4,800]{2,1,0:T(4,128)} async-done(((f32[784,4,800]{2,1,0:T(4,128)}), f32[784,4,800]{2,1,0:T(4,128)}) %all-reduce.9.cloned.1.call-update) | async-done | bytes 10035216 | tf_op jit(solution)/shard_map/while/body/eval_jaxpr/psum | solution.py:44
  2891.4 16.2 multiply_add_fusion.20
  2907.8 15.4 fusion.34
  2984.4 23.1 psum.57
  3007.5 124.2 %all-reduce.9.cloned.1.call-done = f32[784,4,800]{2,1,0:T(4,128)} async-done(((f32[784,4,800]{2,1,0:T(4,128)}), f32[784,4,800]{2,1,0:T(4,128)}) %all-reduce.9.cloned.1.call-update) | async-done | bytes 10035216 | tf_op jit(solution)/shard_map/while/body/eval_jaxpr/psum | solution.py:44
  3131.7 16.2 multiply_add_fusion.20
  3148.0 15.4 fusion.34
  3224.6 23.1 psum.57
  3247.7 124.2 %all-reduce.9.cloned.1.call-done = f32[784,4,800]{2,1,0:T(4,128)} async-done(((f32[784,4,800]{2,1,0:T(4,128)}), f32[784,4,800]{2,1,0:T(4,128)}) %all-reduce.9.cloned.1.call-update) | async-done | bytes 10035216 | tf_op jit(solution)/shard_map/while/body/eval_jaxpr/psum | solution.py:44
  3371.9 16.2 multiply_add_fusion.20
  3388.3 15.4 fusion.34
  3464.9 23.1 psum.57
  3488.0 124.2 %all-reduce.9.cloned.1.call-done = f32[784,4,800]{2,1,0:T(4,128)} async-done(((f32[784,4,800]{2,1,0:T(4,128)}), f32[784,4,800]{2,1,0:T(4,128)}) %all-reduce.9.cloned.1.call-update) | async-done | bytes 10035216 | tf_op jit(solution)/shard_map/while/body/eval_jaxpr/psum | solution.py:44
  3612.2 16.2 multiply_add_fusion.20
  3705.1 23.1 psum.57
  3728.2 124.2 %all-reduce.9.cloned.1.call-done = f32[784,4,800]{2,1,0:T(4,128)} async-done(((f32[784,4,800]{2,1,0:T(4,128)}), f32[784,4,800]{2,1,0:T(4,128)}) %all-reduce.9.cloned.1.call-update) | async-done | bytes 10035216 | tf_op jit(solution)/shard_map/while/body/eval_jaxpr/psum | solution.py:44
  3852.4 16.2 multiply_add_fusion.20
  3953.1 23.1 all-reduce
  3977.0 123.5 %all-reduce.7.cloned.1.call-done = f32[784,4,800]{2,1,0:T(4,128)} async-done(((f32[784,4,800]{2,1,0:T(4,128)}), f32[784,4,800]{2,1,0:T(4,128)}) %all-reduce.7.cloned.1.call-update) | async-done | bytes 10035216 | tf_op jit(solution)/shard_map/psum | solution.py:44
  4100.4 16.8 multiply_reduce_fusion.4
  (332 shorter events, 1130.1 us)
Async XLA Ops:
  7.2 229.3 %all-reduce.5.cloned.1.call-start = ((), (), s32[]{:S(2)}) async-start(), calls=%async_computation | async-start | bytes 22478848 | tf_op jit(solution)/shard_map/psum | solution.py:44
  7.9 10.8 copy-start.8
  27.4 22.6 copy-start.9
  72.5 39.8 copy-start.7
  264.9 15.6 copy-start.2
  264.9 224.1 %all-reduce.9.cloned.1.call-start = ((), (), s32[]{:S(2)}) async-start(), calls=%async_computation.2 | async-start | bytes 22478848 | tf_op jit(solution)/shard_map/while/body/eval_jaxpr/psum | solution.py:44
  300.0 4.7 copy-start
  488.9 16.2 copy-start.3
  505.1 15.6 copy-start.2
  505.1 224.1 %all-reduce.9.cloned.1.call-start = ((), (), s32[]{:S(2)}) async-start(), calls=%async_computation.2 | async-start | bytes 22478848 | tf_op jit(solution)/shard_map/while/body/eval_jaxpr/psum | solution.py:44
  540.2 4.7 copy-start
  729.2 16.2 copy-start.3
  745.4 15.6 copy-start.2
  745.4 224.1 %all-reduce.9.cloned.1.call-start = ((), (), s32[]{:S(2)}) async-start(), calls=%async_computation.2 | async-start | bytes 22478848 | tf_op jit(solution)/shard_map/while/body/eval_jaxpr/psum | solution.py:44
  969.4 16.2 copy-start.3
  985.6 15.6 copy-start.2
  985.6 224.1 %all-reduce.9.cloned.1.call-start = ((), (), s32[]{:S(2)}) async-start(), calls=%async_computation.2 | async-start | bytes 22478848 | tf_op jit(solution)/shard_map/while/body/eval_jaxpr/psum | solution.py:44
  1020.7 4.7 copy-start
  1209.7 16.2 copy-start.3
  1225.9 15.6 copy-start.2
  1225.9 224.1 %all-reduce.9.cloned.1.call-start = ((), (), s32[]{:S(2)}) async-start(), calls=%async_computation.2 | async-start | bytes 22478848 | tf_op jit(solution)/shard_map/while/body/eval_jaxpr/psum | solution.py:44
  1449.9 16.2 copy-start.3
  1466.1 15.6 copy-start.2
  1466.1 224.1 %all-reduce.9.cloned.1.call-start = ((), (), s32[]{:S(2)}) async-start(), calls=%async_computation.2 | async-start | bytes 22478848 | tf_op jit(solution)/shard_map/while/body/eval_jaxpr/psum | solution.py:44
  1501.2 4.7 copy-start
  1690.2 16.2 copy-start.3
  1706.4 15.6 copy-start.2
  1706.4 224.1 %all-reduce.9.cloned.1.call-start = ((), (), s32[]{:S(2)}) async-start(), calls=%async_computation.2 | async-start | bytes 22478848 | tf_op jit(solution)/shard_map/while/body/eval_jaxpr/psum | solution.py:44
  1741.5 4.7 copy-start
  1930.4 16.2 copy-start.3
  1946.6 15.6 copy-start.2
  1946.6 224.1 %all-reduce.9.cloned.1.call-start = ((), (), s32[]{:S(2)}) async-start(), calls=%async_computation.2 | async-start | bytes 22478848 | tf_op jit(solution)/shard_map/while/body/eval_jaxpr/psum | solution.py:44
  1981.7 4.7 copy-start
  2170.7 16.2 copy-start.3
  2186.9 15.6 copy-start.2
  2186.9 224.1 %all-reduce.9.cloned.1.call-start = ((), (), s32[]{:S(2)}) async-start(), calls=%async_computation.2 | async-start | bytes 22478848 | tf_op jit(solution)/shard_map/while/body/eval_jaxpr/psum | solution.py:44
  2222.0 4.7 copy-start
  2410.9 16.2 copy-start.3
  2427.1 15.6 copy-start.2
  2427.1 224.1 %all-reduce.9.cloned.1.call-start = ((), (), s32[]{:S(2)}) async-start(), calls=%async_computation.2 | async-start | bytes 22478848 | tf_op jit(solution)/shard_map/while/body/eval_jaxpr/psum | solution.py:44
  2651.2 16.2 copy-start.3
  2667.4 15.6 copy-start.2
  2667.4 224.1 %all-reduce.9.cloned.1.call-start = ((), (), s32[]{:S(2)}) async-start(), calls=%async_computation.2 | async-start | bytes 22478848 | tf_op jit(solution)/shard_map/while/body/eval_jaxpr/psum | solution.py:44
  2702.5 4.7 copy-start
  2891.4 16.2 copy-start.3
  2907.6 15.6 copy-start.2
  2907.6 224.1 %all-reduce.9.cloned.1.call-start = ((), (), s32[]{:S(2)}) async-start(), calls=%async_computation.2 | async-start | bytes 22478848 | tf_op jit(solution)/shard_map/while/body/eval_jaxpr/psum | solution.py:44
  3131.7 16.2 copy-start.3
  3147.9 15.6 copy-start.2
  3147.9 224.1 %all-reduce.9.cloned.1.call-start = ((), (), s32[]{:S(2)}) async-start(), calls=%async_computation.2 | async-start | bytes 22478848 | tf_op jit(solution)/shard_map/while/body/eval_jaxpr/psum | solution.py:44
  3183.0 4.7 copy-start
  3371.9 16.2 copy-start.3
  3388.1 15.6 copy-start.2
  3388.1 224.1 %all-reduce.9.cloned.1.call-start = ((), (), s32[]{:S(2)}) async-start(), calls=%async_computation.2 | async-start | bytes 22478848 | tf_op jit(solution)/shard_map/while/body/eval_jaxpr/psum | solution.py:44
  3612.2 16.2 copy-start.3
  3628.4 15.6 copy-start.2
  3628.4 224.1 %all-reduce.9.cloned.1.call-start = ((), (), s32[]{:S(2)}) async-start(), calls=%async_computation.2 | async-start | bytes 22478848 | tf_op jit(solution)/shard_map/while/body/eval_jaxpr/psum | solution.py:44
  3663.5 4.7 copy-start
  3852.4 16.2 copy-start.3
  3869.0 14.8 copy-start.4
  3869.0 231.4 %all-reduce.7.cloned.1.call-start = ((), (), s32[]{:S(2)}) async-start(), calls=%async_computation.1 | async-start | bytes 22478848 | tf_op jit(solution)/shard_map/psum | solution.py:44
  3869.2 107.1 %copy-start.6 = (f32[4,800]{1,0:T(4,128)}, f32[4,800]{1,0:T(4,128)S(1)}, u32[]{:S(2)}) copy-start(f32[4,800]{1,0:T(4,128)S(1)} %get-tuple-element.68) | copy-start | bytes 38404
  3911.9 4.7 copy-start.1
  3911.9 5.7 copy-start.5
  (5 other events, 23.3 us)
Sparse Core Ops, SparseCore 0:
  86.3 150.0 all-reduce.4
  341.7 147.2 all-reduce.8
  581.9 147.2 all-reduce.8
  822.2 147.2 all-reduce.8
  1062.4 147.2 all-reduce.8
  1302.7 147.2 all-reduce.8
  1542.9 147.2 all-reduce.8
  1783.2 147.2 all-reduce.8
  2023.4 147.2 all-reduce.8
  2263.7 147.2 all-reduce.8
  2503.9 147.2 all-reduce.8
  2744.2 147.2 all-reduce.8
  2984.4 147.2 all-reduce.8
  3224.7 147.2 all-reduce.8
  3464.9 147.2 all-reduce.8
  3705.1 147.2 all-reduce.8
  3953.2 147.2 all-reduce.6
where the time goes:
time: 4140 us; the launch traced here: 4120 us
  waiting for transfers between devices  2110 us (51%)
  other arithmetic  739 us (18%)
  local copies, waits for them, and re-layouts  504 us (12%)
  blocking collectives  396 us (10%)
  matrix products  347 us (8%)
    psum x17, waiting for transfers between devices, log_post_grad(): grad_in, grad_out = lax.psum((grad_in, grad_out), 'data')  2110 us
    psum x17, blocking collectives, log_post_grad(): grad_in, grad_out = lax.psum((grad_in, grad_out), 'data')  396 us
    convert_element_type x17, other arithmetic, log_post_grad(): w_flat = pos_in.astype(jnp.bfloat16).reshape(num_feat, num_chain * hidden)  249 us
    add x15, other arithmetic, leap_step(): vel_in + step_size * grad_in  243 us
    reshape x17, local copies, waits for them, and re-layouts, local_terms(): grad_in.reshape(w_flat.shape[0], num_chain, hidden)  233 us
    dot_general x17, matrix products, local_terms(): lax.dot_general(x_rows, back_grad.reshape(num_rows, num_chain * hidden),...  184 us
    reduce_sum x17, other arithmetic, local_terms(): grad_out = jnp.sum(hidden_act * residual[:, :, None], axis=0)  172 us
    reshape x17, local copies, waits for them, and re-layouts, log_post_grad(): w_flat = pos_in.astype(jnp.bfloat16).reshape(num_feat, num_chain * hidden)  169 us
  transfers between devices with their start and end apart: 17, of which 17 were waited for; matrix products, arithmetic and copies ran while one was open for 0% of the time, Pallas kernels for 0%

commit v1 on v0

v1 whole, which is shorter than its diff:
```python
import functools
import math
import jax
import jax.numpy as jnp
from jax import lax
from jax.experimental import pallas as pl
from jax.experimental.pallas import tpu as pltpu
from jax.sharding import PartitionSpec as P

LEAPS = 16
PRIOR_VAR = 1.0
MAIN = 768
BLOCK = 2048
CHUNK = 512
DEPTH = 512
MESH = pl.DeviceIdType.MESH
F32 = jnp.float32
BF16 = jnp.bfloat16
NT = (((1,), (1,)), ((), ()))


def chain_kernel(step, xm_hbm, xr_hbm, lab_ref, wm0, wr0, v0, pm0, pr0, q0,
                 wm, wr, v, pm, pr, q, energy,
                 xm, xr, act, bt, gm, gr, g2, wmb, wrb, z_own, z_peer,
                 load_sem, send_sem, recv_sem):
    num_rows = xm.shape[0]
    num_block = num_rows // BLOCK
    me = lax.axis_index("data")
    core = lax.rem(me, 2)
    peer = me + 1 - 2 * core

    barrier = pltpu.get_barrier_semaphore()
    pl.semaphore_signal(barrier, inc=1, device_id={"data": peer}, device_id_type=MESH)
    pl.semaphore_wait(barrier, 1)

    load_m = pltpu.make_async_copy(xm_hbm, xm, load_sem.at[0])
    load_r = pltpu.make_async_copy(xr_hbm, xr, load_sem.at[1])
    load_m.start()
    load_r.start()
    wm[...] = wm0[...]
    wr[...] = wr0[...]
    v[...] = v0[...]
    pm[...] = pm0[...]
    pr[...] = pr0[...]
    q[...] = q0[...]
    wmb[...] = wm0[...].astype(BF16)
    wrb[...] = wr0[...].astype(BF16)
    load_m.wait()
    load_r.wait()

    def z_copy(slot, block):
        span = pl.ds(block * BLOCK, BLOCK)
        return pltpu.make_async_remote_copy(
            src_ref=z_own.at[slot, :, span], dst_ref=z_peer.at[slot, :, span],
            send_sem=send_sem.at[slot, block], recv_sem=recv_sem.at[slot, block],
            device_id={"data": peer}, device_id_type=MESH)

    def forward(block, slot):
        base = block * BLOCK
        for n in range(BLOCK // CHUNK):
            rows = pl.ds(pl.multiple_of(base + n * CHUNK, CHUNK), CHUNK)
            pre = lax.dot_general(wmb[...], xm[rows, :], NT, preferred_element_type=F32)
            pre = pre + jnp.dot(wrb[...], xr[:, rows], preferred_element_type=F32)
            for j in range(CHUNK // 128):
                cols = pl.ds(pl.multiple_of(base + n * CHUNK + j * 128, 128), 128)
                t = jnp.tanh(pre[:, j * 128:(j + 1) * 128])
                act[:, cols] = t
                z_own[slot, :, cols] = jnp.sum(t * v[...], axis=0, keepdims=True)
        z_copy(slot, block).start()

    def backward(block, slot):
        z_copy(slot, block).wait()
        base = block * BLOCK
        for n in range(BLOCK // DEPTH):
            for j in range(DEPTH // 128):
                cols = pl.ds(pl.multiple_of(base + n * DEPTH + j * 128, 128), 128)
                z = z_own[slot, :, cols] + z_peer[slot, :, cols]
                r = lab_ref[:, cols] - jax.nn.sigmoid(z)
                t = act[:, cols]
                rb = jnp.broadcast_to(r, t.shape)
                bt[:, pl.ds(n * DEPTH + j * 128, 128)] = ((rb * v[...]) * (1.0 - t * t)).astype(BF16)
                g2[...] += rb * t
            rows = pl.ds(pl.multiple_of(base + n * DEPTH, DEPTH), DEPTH)
            b = bt[:, n * DEPTH:(n + 1) * DEPTH]
            gm[...] += jnp.dot(b, xm[rows, :], preferred_element_type=F32)
            gr[...] += lax.dot_general(b, xr[:, rows], NT, preferred_element_type=F32)

    def gradient(index, carry):
        slot = lax.rem(index, 2)
        edge = jnp.logical_or(index == 0, index == LEAPS)
        kick = jnp.where(edge, 0.5 * step, step).astype(F32)
        drift = jnp.where(index == LEAPS, 0.0, step).astype(F32)
        gm[...] = jnp.zeros_like(gm)
        gr[...] = jnp.zeros_like(gr)
        g2[...] = jnp.zeros_like(g2)

        def fwd(block, c):
            forward(block, slot)
            return c

        def bwd(block, c):
            backward(block, slot)
            return c

        lax.fori_loop(0, num_block, fwd, 0)
        lax.fori_loop(0, num_block, bwd, 0)

        def update(w, p, g, wb):
            new_p = p[...] + kick * (g - w[...] / PRIOR_VAR)
            p[...] = new_p
            new_w = w[...] + drift * new_p
            w[...] = new_w
            if wb is not None:
                wb[...] = new_w.astype(BF16)

        update(wm, pm, gm[...], wmb)
        update(wr, pr, gr[...], wrb)
        update(v, q, jnp.broadcast_to(jnp.sum(g2[...], axis=1, keepdims=True), g2.shape), None)
        return carry

    lax.fori_loop(0, LEAPS + 1, gradient, 0)
    last = LEAPS % 2
    z = z_own[last] + z_peer[last]
    loss = jnp.maximum(z, 0.0) + jnp.log1p(jnp.exp(-jnp.abs(z))) - lab_ref[...] * z

    def total(x):
        return jnp.sum(jnp.sum(x, axis=0, keepdims=True), axis=1, keepdims=True)

    squares = total(wm[...] * wm[...]) + total(wr[...] * wr[...]) + total(v[...] * v[...]) / 128.0
    moving = total(pm[...] * pm[...]) + total(pr[...] * pr[...]) + total(q[...] * q[...]) / 128.0
    mine = 0.5 * total(loss) + squares / (2.0 * PRIOR_VAR) + 0.5 * moving
    energy[...] = jnp.broadcast_to(mine, energy.shape)


def run_kernel(step, xm, xr, lab, state):
    num_rows = xm.shape[0]
    half = state[0].shape[0]
    vmem = pl.BlockSpec(memory_space=pltpu.VMEM)
    hbm = pl.BlockSpec(memory_space=pl.ANY)
    rest = xr.shape[0]
    shapes = [jax.ShapeDtypeStruct(s.shape, F32) for s in state] + [jax.ShapeDtypeStruct((1, 128), F32)]
    return pl.pallas_call(
        functools.partial(chain_kernel, step),
        out_shape=shapes,
        in_specs=[hbm, hbm] + [vmem] * 7,
        out_specs=[vmem] * 7,
        scratch_shapes=[
            pltpu.VMEM((num_rows, MAIN), BF16),
            pltpu.VMEM((rest, num_rows), BF16),
            pltpu.VMEM((half, num_rows), F32),
            pltpu.VMEM((half, BLOCK), BF16),
            pltpu.VMEM((half, MAIN), F32),
            pltpu.VMEM((half, rest), F32),
            pltpu.VMEM((half, 128), F32),
            pltpu.VMEM((half, MAIN), BF16),
            pltpu.VMEM((half, rest), BF16),
            pltpu.VMEM((2, 1, num_rows), F32),
            pltpu.VMEM((2, 1, num_rows), F32),
            pltpu.SemaphoreType.DMA((2,)),
            pltpu.SemaphoreType.DMA((2, num_rows // BLOCK)),
            pltpu.SemaphoreType.DMA((2, num_rows // BLOCK)),
        ],
        compiler_params=pltpu.CompilerParams(
            collective_id=0, has_side_effects=True, vmem_limit_bytes=60 * 2 ** 20),
    )(xm, xr, lab, *state)


def solution(mesh):
    row_spec = P('data', None)
    label_spec = P('data')
    in_spec = P(None, 'parts', None)
    out_spec = P('parts', None)
    chain_spec = P('parts')

    def run_chains(feats, labels, w_in, w_out, mom_in, mom_out):
        num_rows, num_feat = feats.shape
        hidden = w_in.shape[2]
        chains = w_in.shape[1]
        half = hidden // 2
        step = 1.0 / math.sqrt(num_rows * (num_feat + hidden))

        def device_body(x_rows, y_rows, w1, w2, p1, p2):
            me = lax.axis_index('data')
            chain, core = me // 2, me % 2
            xm = lax.all_gather(x_rows[:, :MAIN], 'data', axis=0, tiled=True)
            xr = lax.all_gather(x_rows[:, MAIN:].T, 'data', axis=0)
            xr = jnp.moveaxis(xr, 0, 1).reshape(num_feat - MAIN, num_rows)
            lab = lax.all_gather(y_rows, 'data', axis=0, tiled=True).astype(F32)[None, :]

            def mine_in(w):
                w = lax.dynamic_slice(w, (0, chain, core * half), (num_feat, 1, half))[:, 0, :].T
                return w[:, :MAIN], w[:, MAIN:]

            def mine_out(u):
                u = lax.dynamic_slice(u, (chain, core * half), (1, half))
                return jnp.broadcast_to(u.T, (half, 128))

            state = (*mine_in(w1), mine_out(w2), *mine_in(p1), mine_out(p2))
            wm, wr, v, pm, pr, q, energy = run_kernel(step, xm, xr, lab, state)

            def all_in(m, r):
                mine = jnp.concatenate([m, r], axis=1).T
                every = lax.all_gather(mine, 'data', axis=0)
                every = every.reshape(chains, 2, num_feat, half)
                return jnp.transpose(every, (2, 0, 1, 3)).reshape(num_feat, chains, hidden)

            def all_out(u):
                return lax.all_gather(u[:, 0], 'data', axis=0).reshape(chains, hidden)

            total = lax.all_gather(energy[0, :1], 'data', axis=0).reshape(chains, 2).sum(axis=1)
            return all_in(wm, wr), all_out(v), all_in(pm, pr), all_out(q), total

        mapped = jax.shard_map(device_body, mesh=mesh, in_specs=(row_spec, label_spec, in_spec, out_spec, in_spec, out_spec), out_specs=(in_spec, out_spec, in_spec, out_spec, chain_spec), check_vma=False)
        return mapped(feats, labels, w_in, w_out, mom_in, mom_out)

    return run_chains
```

time: 4140 us -> 550 us (0.13)
  waiting for transfers between devices: 2110 us -> 99.3 us
  other arithmetic: 739 us -> 5.13 us
  local copies, waits for them, and re-layouts: 504 us -> 65.9 us
  matrix products: 347 us -> 0 us
  blocking collectives: 396 us -> 51 us
  Pallas kernels: 0 us -> 314 us
    psum x17 -> x0, waiting for transfers between devices: 2110 us -> none  [log_post_grad(): grad_in, grad_out = lax.psum((grad_in, grad_out), 'data')]
    reshape x34 -> x3, local copies, waits for them, and re-layouts: 403 us -> 1.45 us  [the longest x2 1.36 us: all_out(): return lax.all_gather(u[:, 0], 'data', axis=0).reshape(chains, hidden)]
    psum x17 -> x0, blocking collectives: 396 us -> none  [log_post_grad(): grad_in, grad_out = lax.psum((grad_in, grad_out), 'data')]
    dot_general x34 -> x0, matrix products: 347 us -> none  [the longest x17 184 us: local_terms(): lax.dot_general(x_rows, back_grad.reshape(num_rows, num_chain * hidden),...]
    pallas_call x0 -> x1, Pallas kernels: none -> 314 us  [run_kernel(): pl.pallas_call(functools.partial(chain_kernel, step), out_shape=shapes, i...]
    add x48 -> x0, other arithmetic: 260 us -> none  [the longest x15 243 us: leap_step(): vel_in + step_size * grad_in]
    convert_element_type x18 -> x1, other arithmetic: 249 us -> 0.62 us  [device_body(): lax.all_gather(y_rows, 'data', axis=0, tiled=True).astype(F32)[None, :]]
    reduce_sum x38 -> x1, other arithmetic: 220 us -> 0.63 us  [device_body(): lax.all_gather(energy[0, :1], 'data', axis=0).reshape(chains, 2).sum(axis=1)]
  transfers between devices with their start and end apart: 17 -> 3, of which waited for: 17 -> 3; matrix products, arithmetic and copies ran while one was open for 0% -> 9% of each run, Pallas kernels for 0% -> 0%
where the time goes in v1:
time: 550 us; the launch traced here: 549 us
  Pallas kernels  314 us (57%)
  waiting for transfers between devices  99.3 us (18%)
  local copies, waits for them, and re-layouts  65.9 us (12%)
  blocking collectives  51 us (9%)
  between operations  14 us (3%)
    pallas_call x1, Pallas kernels, run_kernel(): pl.pallas_call(functools.partial(chain_kernel, step), out_shape=shapes, i...  314 us
    all_gather x2, waiting for transfers between devices, all_in(): every = lax.all_gather(mine, 'data', axis=0)  81.6 us
    unnamed x24, local copies, waits for them, and re-layouts  36.6 us
    unnamed x1, blocking collectives  23.2 us
    all_gather x1, waiting for transfers between devices, device_body(): xm = lax.all_gather(x_rows[:, :MAIN], 'data', axis=0, tiled=True)  17.6 us
    dynamic_slice x3, local copies, waits for them, and re-layouts, mine_in(): lax.dynamic_slice(w, (0, chain, core * half), (num_feat, 1, half))[:, 0, :]  17.2 us
    all_gather x1, blocking collectives, device_body(): lax.all_gather(y_rows, 'data', axis=0, tiled=True).astype(F32)[None, :]  14.2 us
    all_gather x1, blocking collectives, device_body(): xr = lax.all_gather(x_rows[:, MAIN:].T, 'data', axis=0)  13.6 us
  transfers between devices with their start and end apart: 3, of which 3 were waited for; matrix products, arithmetic and copies ran while one was open for 9% of the time, Pallas kernels for 0%

profile of v1, /device:TPU:0, one launch (start us, length us, event | category | flops | bytes accessed | tf_op | source)
XLA Modules:
  0.0 548.9 jit_solution(4315917033953394461)
XLA Ops:
  7.2 0.0 slice-start
  7.2 0.0 all-gather.11.cloned.1.call-start
  7.2 1.4 slice-done
  8.6 1.6 copy.29
  10.1 0.0 all-gather.11.cloned.1.call-update
  10.2 0.0 all-gather.13.cloned.1.call-start
  10.2 12.2 %constant_dynamic-slice_fusion = (f32[784,1,400]{2,1,0:T(1,128)S(1)}, f32[784,1,400]{2,1,0:T(1,128)S(1)}) fusion(f32[784,4,800]{2,1,0:T(4,128)} %param.10, s32[]{:T(128)S(6)} %select_n.24, s32[]{:T(128)S(6)} %select_n.26, f32[784,4,800]{2,1,0:T(4,128)} %param.8), kind=kLoop, calls=%fused_computation.6 | loop fusion | bytes 5017608 | tf_op jit(solution)/shard_map/dynamic_slice | solution.py:191
  22.5 3.5 copy.26
  26.0 1.6 slice.39.pr0
  27.6 2.4 slice.38.pm0
  30.0 1.4 copy.25
  31.5 0.0 copy-start.5
  31.5 0.0 copy-start
  31.5 0.7 slice.37.wr0
  32.2 1.1 slice.36.wm0
  33.3 0.8 dynamic_slice.13
  34.1 0.8 dynamic_slice.15
  34.9 0.0 copy-done.5
  34.9 14.2 %all_gather.36 = s32[8192]{0:T(1024)S(1)} all-gather(s32[1024]{0:T(1024)S(1)} %copy-done.5), channel_id=1, replica_groups=mesh['parts'=1,'data'=8] {'data'}, dimensions={0}, use_global_device_ids=true | all-gather | bytes 36864 | tf_op jit(solution)/shard_map/all_gather | solution.py:188
  49.1 0.6 convert_element_type.3
  49.7 0.0 copy-done
  49.7 13.6 %all-gather = bf16[128,1024]{1,0:T(8,128)(2,1)S(1)} all-gather(bf16[16,1024]{1,0:T(8,128)(2,1)S(1)} %slice_bitcast_fusion), channel_id=2, replica_groups=mesh['parts'=1,'data'=8] {'data'}, dimensions={0}, use_global_device_ids=true | all-gather | bytes 294912 | tf_op jit(solution)/shard_map/all_gather | solution.py:186
  63.3 0.7 copy.30
  64.0 17.6 %all-gather.11.cloned.1.call-done.xm_hbm = bf16[8192,768]{1,0:T(8,128)(2,1)} async-done(((bf16[1024,768]{1,0:T(8,128)(2,1)}), bf16[8192,768]{1,0:T(8,128)(2,1)}) %all-gather.11.cloned.1.call-update) | async-done | bytes 12582928 | tf_op jit(solution)/shard_map/all_gather | solution.py:185
  81.6 0.8 broadcast_in_dim.21.q0
  82.5 0.8 broadcast_in_dim.19.v0
  83.3 313.5 %shard_map.101 = (f32[400,768]{1,0:T(8,128)}, f32[400,16]{1,0:T(8,128)}, f32[400,128]{1,0:T(8,128)}, f32[400,768]{1,0:T(8,128)}, f32[400,16]{1,0:T(8,128)}, /*index=5*/f32[400,128]{1,0:T(8,128)}, f32[1,128]{1,0:T(1,128)}) custom-call(bf16[8192,768]{1,0:T(8,128)(2,1)} %all-gather.11.cloned.1.call-done.xm_hbm, bf16[16,8192]{1,0:T(8,128)(2,1)} %bitcast.44, ...), custom_call_target="tpu_custom_call" | custom-call | tf_op jit(solution)/shard_map/pallas_call | solution.py:142
  396.8 0.0 copy-start.1
  396.8 0.0 copy-start.2
  396.8 2.7 maximum_bitcast_fusion
  399.5 0.0 all-gather.13.cloned.1.call-update
  399.5 0.0 all-gather.15.cloned.1.call-start
  399.6 0.0 copy-done.1
  399.6 0.0 copy-done.2
  399.6 0.0 copy-start.6
  399.6 0.0 copy-start.4
  399.6 0.0 copy-start.3
  399.6 1.2 maximum_bitcast_fusion.1
  400.8 0.0 all-gather.15.cloned.1.call-update
  400.9 0.0 copy-done.6
  400.9 0.1 bitcast_dynamic-update-slice_fusion
  400.9 0.0 copy-done.4
  400.9 0.1 slice_reduce_fusion.1
  401.1 0.3 dynamic-update-slice
  401.4 0.0 copy-done.3
  401.4 0.1 slice_reduce_fusion
  401.5 0.3 dynamic-update-slice.1
  401.8 23.2 %all-reduce.3 = (f32[3200]{0:T(1024)S(1)}, f32[3200]{0:T(1024)S(1)}, f32[8]{0:T(128)S(1)}) all-reduce(f32[3200]{0:T(1024)S(1)} %dynamic-update-slice, f32[3200]{0:T(1024)S(1)} %dynamic-update-slice.1, f32[8]{0:T(128)S(1)} %bitcast_dynamic-update-slice_fusion), channel_id=4, replica_groups=mesh['parts'=1,'data'=8] {'data'}, use_global_device_ids=true, to_apply=%add | all-reduce | flops 6408 | bytes 51264
  425.0 0.7 reshape.39
  425.7 0.1 reshape.43
  425.8 0.7 reshape.42
  426.4 0.6 reduce_sum.9
  427.1 35.0 %all-gather.13.cloned.1.call-done = f32[8,784,400]{1,2,0:T(8,128)} async-done(((f32[1,784,400]{1,2,0:T(8,128)}), f32[8,784,400]{1,2,0:T(8,128)}) %all-gather.13.cloned.1.call-update) | async-done | bytes 10035216 | tf_op jit(solution)/shard_map/all_gather | solution.py:203
  462.1 16.8 %copy.27 = f32[784,4,800]{2,1,0:T(4,128)} copy(f32[784,4,800]{0,2,1:T(8,128)} %bitcast.38) | data formatting | bytes 20070400
  479.0 46.6 %all-gather.15.cloned.1.call-done = f32[8,784,400]{1,2,0:T(8,128)} async-done(((f32[1,784,400]{1,2,0:T(8,128)}), f32[8,784,400]{1,2,0:T(8,128)}) %all-gather.15.cloned.1.call-update) | async-done | bytes 10035216 | tf_op jit(solution)/shard_map/all_gather | solution.py:203
  525.5 16.8 %copy.28 = f32[784,4,800]{2,1,0:T(4,128)} copy(f32[784,4,800]{0,2,1:T(8,128)} %bitcast.39) | data formatting | bytes 20070400
  (4 shorter events, 0.0 us)
Async XLA Ops:
  7.2 1.4 slice-start
  7.2 74.5 %all-gather.11.cloned.1.call-start = ((), (), s32[]{:S(2)}) async-start(), calls=%async_computation | async-start | bytes 14155776 | tf_op jit(solution)/shard_map/all_gather | solution.py:185
  10.2 452.0 %all-gather.13.cloned.1.call-start = ((), (), s32[]{:S(2)}) async-start(), calls=%async_computation.1 | async-start | bytes 12902400 | tf_op jit(solution)/shard_map/all_gather | solution.py:203
  31.5 3.4 copy-start.5
  31.5 18.2 %copy-start = (bf16[1024,784]{0,1:T(8,128)(2,1)S(1)}, bf16[1024,784]{0,1:T(8,128)(2,1)}, u32[]{:S(2)}) copy-start(bf16[1024,784]{0,1:T(8,128)(2,1)} %param.6) | copy-start | bytes 4816900
  396.8 2.8 copy-start.1
  396.8 2.8 copy-start.2
  399.5 126.0 %all-gather.15.cloned.1.call-start = ((), (), s32[]{:S(2)}) async-start(), calls=%async_computation.2 | async-start | bytes 12902400 | tf_op jit(solution)/shard_map/all_gather | solution.py:203
  399.6 1.3 copy-start.6
  399.6 1.3 copy-start.4
  399.6 1.8 copy-start.3
Sparse Core Ops, SparseCore 0:
  10.4 71.2 all-gather.10
  399.6 62.4 all-gather.12
  463.9 61.5 all-gather.14

commit v2 on v1

v2 whole, which is shorter than its diff:
```python
import functools
import math
import jax
import jax.numpy as jnp
from jax import lax
from jax.experimental import pallas as pl
from jax.experimental.pallas import tpu as pltpu
from jax.sharding import PartitionSpec as P

LEAPS = 16
PRIOR_VAR = 1.0
MAIN = 768
BLOCK = 2048
CHUNK = 512
DEPTH = 512
PIECE = 512
SMALL = 24
MESH = pl.DeviceIdType.MESH
F32 = jnp.float32
BF16 = jnp.bfloat16
NT = (((1,), (1,)), ((), ()))


def chain_kernel(step, x_hbm, xr_ref, lab_ref, w1_hbm, w2_ref, p1_hbm, p2_ref,
                 end_w, end_ws, end_p, end_ps,
                 xm, xr, lab, stage, turn, act, bt, gm, gr, g2, wm, wr, v, pm, pr, q, wmb, wrb,
                 z_own, z_peer, small_w, small_p,
                 load_sem, x_send, x_recv, send_sem, recv_sem, end_send, end_recv, end_load):
    num_rows = xm.shape[0]
    num_block = num_rows // BLOCK
    half = wm.shape[0]
    rest = xr.shape[0]
    me = lax.axis_index("data")
    chip = me // 2
    core = lax.rem(me, 2)
    x_bit = lax.rem(chip, 2)
    y_bit = chip // 2
    peer = me + 1 - 2 * core
    x_near = me + 2 - 4 * x_bit
    y_near = me + 4 - 8 * y_bit
    far = x_near + 4 - 8 * y_bit

    barrier = pltpu.get_barrier_semaphore()
    for other in (peer, x_near, y_near):
        pl.semaphore_signal(barrier, inc=1, device_id={"data": other}, device_id_type=MESH)

    def rows_of(position, size):
        return pl.ds(pl.multiple_of(position * size, size), size)

    own = [2 * core, 2 * core + 1]
    mine = rows_of(core, 2 * PIECE)
    loads = [
        pltpu.make_async_copy(x_hbm.at[:, pl.ds(0, MAIN)], xm.at[mine, :], load_sem.at[0]),
        pltpu.make_async_copy(xr_ref, xr.at[:, mine], load_sem.at[1]),
        pltpu.make_async_copy(lab_ref, lab.at[:, mine], load_sem.at[2]),
    ]
    for c in loads:
        c.start()
    load_w = pltpu.make_async_copy(w1_hbm, stage, load_sem.at[3])
    load_p = pltpu.make_async_copy(p1_hbm, stage, load_sem.at[4])
    load_w.start()
    pl.semaphore_wait(barrier, 3)
    for c in loads:
        c.wait()

    def x_copies(src, dst, device, ticket):
        a, b = rows_of(src, PIECE), rows_of(dst, PIECE)
        pairs = ((xm.at[a, :], xm.at[b, :]), (xr.at[:, a], xr.at[:, b]), (lab.at[:, a], lab.at[:, b]))
        return [pltpu.make_async_remote_copy(
            src_ref=s, dst_ref=d, send_sem=x_send.at[i, ticket], recv_sem=x_recv.at[i, dst],
            device_id={"data": device}, device_id_type=MESH) for i, (s, d) in enumerate(pairs)]

    def x_go(src, dst, device, ticket):
        for c in x_copies(src, dst, device, ticket):
            c.start()

    def x_arrived(position):
        for c in x_copies(position, position, peer, 0):
            c.wait_recv()

    def x_sent(ticket):
        for c in x_copies(0, 0, peer, ticket):
            c.wait_send()

    def near_pos(h, which, owner):
        return 4 + 4 * h + 2 * which + owner

    def far_pos(h, owner):
        return 12 + 2 * h + owner

    for h in range(2):
        x_go(own[h], near_pos(h, 0, core), x_near, 3 * h)
        x_go(own[h], near_pos(h, 1, core), y_near, 3 * h + 1)
        x_go(own[h], own[h], peer, 3 * h + 2)

    def part_of(w, m, r, as_bf16):
        for d in range(MAIN // 128):
            turn[:, d * 128:(d + 1) * 128] = stage[d * 128:(d + 1) * 128, chip, :].T
        span = pl.ds(pl.multiple_of(core * half, 8), half)
        m[...] = turn[span, :]
        tail = stage[MAIN:MAIN + rest, chip, :]
        tail = jnp.concatenate([tail, jnp.zeros((128 - rest, tail.shape[1]), F32)], axis=0)
        turn[:, 0:128] = tail.T
        r[...] = turn[span, 0:rest]

    def row_of(u, out):
        turn[:, 0:128] = jnp.broadcast_to(u[pl.ds(chip, 1), :], (128, u.shape[1])).T
        out[...] = turn[pl.ds(pl.multiple_of(core * half, 8), half), 0:128]

    load_w.wait()
    part_of(None, wm, wr, True)
    load_p.start()
    row_of(w2_ref, v)
    wmb[...] = wm[...].astype(BF16)
    wrb[...] = wr[...].astype(BF16)
    row_of(p2_ref, q)
    load_p.wait()
    part_of(None, pm, pr, False)

    other = 1 - core
    x_arrived(2 * other)
    x_arrived(2 * other + 1)

    def arrivals(k):
        if k == 1:
            for which in range(2):
                x_arrived(near_pos(0, which, core))
                if which == 0:
                    x_go(near_pos(0, 0, core), far_pos(0, core), y_near, 6)
                x_go(near_pos(0, which, core), near_pos(0, which, core), peer, 7 + which)
            for which in range(2):
                x_arrived(near_pos(0, which, other))
        elif k == 2:
            for which in (1, 0):
                x_arrived(near_pos(1, which, core))
                if which == 1:
                    x_go(near_pos(1, 1, core), far_pos(1, core), x_near, 9)
                x_go(near_pos(1, which, core), near_pos(1, which, core), peer, 10 + which)
            for which in range(2):
                x_arrived(near_pos(1, which, other))
        elif k == 3:
            for h in range(2):
                x_arrived(far_pos(h, core))
                x_go(far_pos(h, core), far_pos(h, core), peer, 12 + h)
            for h in range(2):
                x_arrived(far_pos(h, other))

    def z_copy(slot, block):
        span = rows_of(block, BLOCK)
        return pltpu.make_async_remote_copy(
            src_ref=z_own.at[slot, :, span], dst_ref=z_peer.at[slot, :, span],
            send_sem=send_sem.at[slot, block], recv_sem=recv_sem.at[slot, block],
            device_id={"data": peer}, device_id_type=MESH)

    def forward(block, slot):
        base = block * BLOCK
        for n in range(BLOCK // CHUNK):
            rows = pl.ds(pl.multiple_of(base + n * CHUNK, CHUNK), CHUNK)
            pre = lax.dot_general(wmb[...], xm[rows, :], NT, preferred_element_type=F32)
            pre = pre + jnp.dot(wrb[...], xr[:, rows], preferred_element_type=F32)
            for j in range(CHUNK // 128):
                cols = pl.ds(pl.multiple_of(base + n * CHUNK + j * 128, 128), 128)
                t = jnp.tanh(pre[:, j * 128:(j + 1) * 128])
                act[:, cols] = t
                z_own[slot, :, cols] = jnp.sum(t * v[...], axis=0, keepdims=True)
        z_copy(slot, block).start()

    def backward(block, slot):
        z_copy(slot, block).wait()
        base = block * BLOCK
        for n in range(BLOCK // DEPTH):
            for j in range(DEPTH // 128):
                cols = pl.ds(pl.multiple_of(base + n * DEPTH + j * 128, 128), 128)
                z = z_own[slot, :, cols] + z_peer[slot, :, cols]
                r = lab[:, cols] - jax.nn.sigmoid(z)
                t = act[:, cols]
                rb = jnp.broadcast_to(r, t.shape)
                bt[:, pl.ds(n * DEPTH + j * 128, 128)] = ((rb * v[...]) * (1.0 - t * t)).astype(BF16)
                g2[...] += rb * t
            rows = pl.ds(pl.multiple_of(base + n * DEPTH, DEPTH), DEPTH)
            b = bt[:, n * DEPTH:(n + 1) * DEPTH]
            gm[...] += jnp.dot(b, xm[rows, :], preferred_element_type=F32)
            gr[...] += lax.dot_general(b, xr[:, rows], NT, preferred_element_type=F32)

    big = (wm, pm)
    small = (small_w, small_p)
    out_big = (end_w, end_p)
    out_small = (end_ws, end_ps)
    part = half // 2

    def end_pair(t, piece, source):
        if piece == 2:
            return small[t], out_small[t].at[source]
        span = pl.ds(piece * part, part)
        return big[t].at[span, :], out_big[t].at[source, span, :]

    def end_copy(t, piece, source, device, ticket, first):
        src, dst = end_pair(t, piece, source)
        return pltpu.make_async_remote_copy(
            src_ref=src if first else dst, dst_ref=dst,
            send_sem=end_send.at[t, piece, ticket], recv_sem=end_recv.at[t, piece, source],
            device_id={"data": device}, device_id_type=MESH)

    def end_arrived(t, piece, source):
        end_copy(t, piece, source, peer, 0, False).wait_recv()

    def end_begin(t):
        for piece in (0, 2, 1):
            end_copy(t, piece, me, x_near, 0, True).start()
            end_copy(t, piece, me, y_near, 1, True).start()
        for piece in (0, 1, 2):
            end_copy(t, piece, me, peer, 2, True).start()
            src, dst = end_pair(t, piece, me)
            pltpu.make_async_copy(src, dst, end_load.at[t, piece]).start()

    def end_relay(t):
        for piece in (0, 2, 1):
            end_arrived(t, piece, x_near)
            if piece != 1:
                end_copy(t, piece, x_near, y_near, 3, False).start()
            end_arrived(t, piece, y_near)
            if piece == 1:
                end_copy(t, piece, y_near, x_near, 3, False).start()
            end_copy(t, piece, x_near, peer, 4, False).start()
            end_copy(t, piece, y_near, peer, 5, False).start()

    def end_finish(t):
        for piece in (0, 2, 1):
            end_arrived(t, piece, far)
            end_copy(t, piece, far, peer, 6, False).start()
        for piece in (0, 1, 2):
            for delta in (me, x_near, y_near, far):
                end_arrived(t, piece, delta + 1 - 2 * core)
            for ticket in range(7):
                end_copy(t, piece, me, peer, ticket, False).wait_send()
            src, dst = end_pair(t, piece, me)
            pltpu.make_async_copy(src, dst, end_load.at[t, piece]).wait()

    def pack_small(buf, r, u, extra):
        wide = jnp.concatenate([r[...], u[:, 0:8], jnp.zeros((half, 104), F32)], axis=1)
        flat = wide.T
        buf[0:rest, :] = flat[0:rest, :]
        buf[rest:SMALL, :] = jnp.where(lax.broadcasted_iota(jnp.int32, (SMALL - rest, half), 0) == 0, flat[rest:SMALL, :], extra)

    def gradient(index, carry):
        slot = lax.rem(index, 2)
        edge = jnp.logical_or(index == 0, index == LEAPS)
        kick = jnp.where(edge, 0.5 * step, step).astype(F32)
        gm[...] = jnp.zeros_like(gm)
        gr[...] = jnp.zeros_like(gr)
        g2[...] = jnp.zeros_like(g2)

        def stage_of(k, c):
            for j in range(1, num_block):
                @pl.when(jnp.logical_and(index == 0, k == j))
                def _():
                    arrivals(j)

            @pl.when(k < num_block)
            def _():
                forward(k, slot)

            @pl.when(k > 0)
            def _():
                backward(k - 1, slot)
            return c

        lax.fori_loop(0, num_block + 1, stage_of, 0)

        pm[...] += kick * (gm[...] - wm[...] / PRIOR_VAR)
        pr[...] += kick * (gr[...] - wr[...] / PRIOR_VAR)
        q[...] += kick * (jnp.broadcast_to(jnp.sum(g2[...], axis=1, keepdims=True), g2.shape) - v[...] / PRIOR_VAR)

        @pl.when(index < LEAPS)
        def _():
            new = wm[...] + step * pm[...]
            wm[...] = new
            wmb[...] = new.astype(BF16)
            new = wr[...] + step * pr[...]
            wr[...] = new
            wrb[...] = new.astype(BF16)
            v[...] += step * q[...]

        @pl.when(index == LEAPS - 1)
        def _():
            pack_small(small_w, wr, v, 0.0)
            end_begin(0)
        return carry

    lax.fori_loop(0, LEAPS + 1, gradient, 0)

    last = LEAPS % 2
    z = z_own[last] + z_peer[last]
    loss = jnp.maximum(z, 0.0) + jnp.log1p(jnp.exp(-jnp.abs(z))) - lab[...] * z

    def total(x):
        return jnp.sum(jnp.sum(x, axis=0, keepdims=True), axis=1, keepdims=True)

    squares = total(wm[...] * wm[...]) + total(wr[...] * wr[...]) + total(v[...] * v[...]) / 128.0
    moving = total(pm[...] * pm[...]) + total(pr[...] * pr[...]) + total(q[...] * q[...]) / 128.0
    energy = 0.5 * total(loss) + squares / (2.0 * PRIOR_VAR) + 0.5 * moving
    pack_small(small_p, pr, q, energy)
    end_begin(1)
    end_relay(0)
    end_relay(1)
    end_finish(0)
    end_finish(1)
    for ticket in range(14):
        x_sent(ticket)


def run_kernel(step, xs, xr, lab, w1, w2, p1, p2, devices):
    num_feat, chains, hidden = w1.shape
    num_rows = xs.shape[0] * devices
    half = hidden // 2
    rest = num_feat - MAIN
    vmem = pl.BlockSpec(memory_space=pltpu.VMEM)
    hbm = pl.BlockSpec(memory_space=pl.ANY)
    big = jax.ShapeDtypeStruct((devices, half, MAIN), F32)
    small = jax.ShapeDtypeStruct((devices, SMALL, half), F32)
    blocks = num_rows // BLOCK
    dma = pltpu.SemaphoreType.DMA
    return pl.pallas_call(
        functools.partial(chain_kernel, step),
        out_shape=[big, small, big, small],
        in_specs=[hbm, hbm, hbm, hbm, vmem, hbm, vmem],
        out_specs=[hbm] * 4,
        scratch_shapes=[
            pltpu.VMEM((num_rows, MAIN), BF16),
            pltpu.VMEM((rest, num_rows), BF16),
            pltpu.VMEM((1, num_rows), F32),
            pltpu.VMEM((num_feat, chains, hidden), F32),
            pltpu.VMEM((hidden, MAIN), F32),
            pltpu.VMEM((half, num_rows), F32),
            pltpu.VMEM((half, BLOCK), BF16),
            pltpu.VMEM((half, MAIN), F32),
            pltpu.VMEM((half, rest), F32),
            pltpu.VMEM((half, 128), F32),
            pltpu.VMEM((half, MAIN), F32),
            pltpu.VMEM((half, rest), F32),
            pltpu.VMEM((half, 128), F32),
            pltpu.VMEM((half, MAIN), F32),
            pltpu.VMEM((half, rest), F32),
            pltpu.VMEM((half, 128), F32),
            pltpu.VMEM((half, MAIN), BF16),
            pltpu.VMEM((half, rest), BF16),
            pltpu.VMEM((2, 1, num_rows), F32),
            pltpu.VMEM((2, 1, num_rows), F32),
            pltpu.VMEM((SMALL, half), F32),
            pltpu.VMEM((SMALL, half), F32),
            dma((5,)),
            dma((3, 14)),
            dma((3, 16)),
            dma((2, blocks)),
            dma((2, blocks)),
            dma((2, 3, 7)),
            dma((2, 3, devices)),
            dma((2, 3)),
        ],
        compiler_params=pltpu.CompilerParams(
            collective_id=0, has_side_effects=True, vmem_limit_bytes=62 * 2 ** 20),
    )(xs, xr, lab, w1, w2, p1, p2)


def place_kernel(gw, gws, gp, gps, end_w, end_p):
    step = pl.program_id(0)
    tiles = MAIN // 128
    chains = end_w.shape[1]
    rest = gws.shape[1] - 8

    @pl.when(step < tiles)
    def _():
        for g, end in ((gw, end_w), (gp, end_p)):
            for c in range(chains):
                end[:, c, :] = jnp.concatenate([g[2 * c], g[2 * c + 1]], axis=0).T

    @pl.when(step == tiles)
    def _():
        for g, end in ((gws, end_w), (gps, end_p)):
            for c in range(chains):
                end[0:rest, c, :] = jnp.concatenate([g[2 * c, 0:rest, :], g[2 * c + 1, 0:rest, :]], axis=1)


def place(gw, gws, gp, gps, num_feat, chains, hidden):
    tiles = MAIN // 128
    devices, half = gw.shape[0], gw.shape[1]
    big = pl.BlockSpec((devices, half, 128), lambda i: (0, 0, jnp.minimum(i, tiles - 1)))
    small = pl.BlockSpec(gws.shape, lambda i: (0, 0, 0))
    out = pl.BlockSpec((128, chains, hidden), lambda i: (i, 0, 0))
    shape = jax.ShapeDtypeStruct((num_feat, chains, hidden), F32)
    return pl.pallas_call(
        place_kernel, grid=(tiles + 1,), out_shape=[shape, shape],
        in_specs=[big, small, big, small], out_specs=[out, out],
        compiler_params=pltpu.CompilerParams(vmem_limit_bytes=48 * 2 ** 20),
    )(gw, gws, gp, gps)


def solution(mesh):
    row_spec = P('data', None)
    label_spec = P('data')
    in_spec = P(None, 'parts', None)
    out_spec = P('parts', None)
    chain_spec = P('parts')
    devices = mesh.shape['data']

    def run_chains(feats, labels, w_in, w_out, mom_in, mom_out):
        num_rows, num_feat = feats.shape
        chains, hidden = w_out.shape
        step = 1.0 / math.sqrt(num_rows * (num_feat + hidden))

        def device_body(x_rows, y_rows, w1, w2, p1, p2):
            xr = x_rows[:, MAIN:].T
            lab = y_rows.astype(F32)[None, :]
            gw, gws, gp, gps = run_kernel(step, x_rows, xr, lab, w1, w2, p1, p2, devices)
            end_w, end_p = place(gw, gws, gp, gps, num_feat, chains, hidden)
            rest = num_feat - MAIN
            end_w2 = gws[:, rest, :].reshape(chains, hidden)
            end_p2 = gps[:, rest, :].reshape(chains, hidden)
            energy = gps[:, rest + 1, 0].reshape(chains, 2).sum(axis=1)
            return end_w, end_w2, end_p, end_p2, energy

        mapped = jax.shard_map(device_body, mesh=mesh, in_specs=(row_spec, label_spec, in_spec, out_spec, in_spec, out_spec), out_specs=(in_spec, out_spec, in_spec, out_spec, chain_spec), check_vma=False)
        return mapped(feats, labels, w_in, w_out, mom_in, mom_out)

    return run_chains
```

time: 550 us -> 463 us (0.84)
  Pallas kernels: 314 us -> 450 us
  waiting for transfers between devices: 99.3 us -> 0 us
  local copies, waits for them, and re-layouts: 65.9 us -> 9.49 us
  blocking collectives: 51 us -> 0 us
  between operations: 14 us -> 0.66 us
    pallas_call x1 -> x2, Pallas kernels: 314 us -> 450 us  [the longest x1 432 us: run_kernel(): pl.pallas_call(functools.partial(chain_kernel, step), out_shape=[big, sma...]
    all_gather x3 -> x0, waiting for transfers between devices: 99.2 us -> none  [the longest x2 81.6 us: all_in(): every = lax.all_gather(mine, 'data', axis=0)]
    unnamed x24 -> x5, local copies, waits for them, and re-layouts: 36.6 us -> 5.69 us
    all_gather x2 -> x0, blocking collectives: 27.8 us -> none  [the longest x1 14.2 us: device_body(): lax.all_gather(y_rows, 'data', axis=0, tiled=True).astype(F32)[None, :]]
    unnamed x1 -> x0, blocking collectives: 23.2 us -> none
    dynamic_slice x5 -> x0, local copies, waits for them, and re-layouts: 18.8 us -> none  [the longest x3 17.2 us: mine_in(): lax.dynamic_slice(w, (0, chain, core * half), (num_feat, 1, half))[:, 0, :]]
    slice x8 -> x2, local copies, waits for them, and re-layouts: 7.46 us -> 0.98 us  [the longest x1 0.9 us: device_body(): energy = gps[:, rest + 1, 0].reshape(chains, 2).sum(axis=1)]
  transfers between devices with their start and end apart: 3 -> 0, of which waited for: 3 -> 0; matrix products, arithmetic and copies ran while one was open for 9% -> 0% of each run, Pallas kernels for 0% -> 0%
where the time goes in v2:
time: 463 us; the launch traced here: 462 us
  Pallas kernels  450 us (97%)
  local copies, waits for them, and re-layouts  9.49 us (2%)
    pallas_call x1, Pallas kernels, run_kernel(): pl.pallas_call(functools.partial(chain_kernel, step), out_shape=[big, sma...  432 us
    pallas_call x1, Pallas kernels, place(): pl.pallas_call(place_kernel, grid=(tiles + 1,), out_shape=[shape, shape],...  18.3 us

profile of v2, /device:TPU:0, one launch (start us, length us, event | category | flops | bytes accessed | tf_op | source)
XLA Modules:
  0.0 462.3 jit_solution(3868996289402931145)
XLA Ops:
  0.6 3.7 copy.12.x_hbm
  4.3 1.4 slice_bitcast_fusion.xr_ref
  5.7 1.3 convert_element_type.3
  7.0 431.9 %shard_map.101 = (f32[8,400,768]{2,1,0:T(8,128)}, f32[8,24,400]{2,1,0:T(8,128)}, f32[8,400,768]{2,1,0:T(8,128)}, f32[8,24,400]{2,1,0:T(8,128)}) custom-call(bf16[1024,784]{1,0:T(8,128)(2,1)} %copy.12.x_hbm, bf16[16,1024]{1,0:T(8,128)(2,1)} %slice_bitcast_fusion.xr_ref, f32[1,1024]{1,0:T(1,128)} %bitcast.3, f32[784,4,800]{2,1,0:T(4,128)} %w1_hbm.1, ...), custom_call_target="tpu_custom_call" | custom-call | tf_op jit(solution)/shard_map/pallas_call | solution.py:323
  438.9 0.0 copy-start
  438.9 1.0 copy-done
  439.9 0.0 copy-start.1
  439.9 1.0 copy-done.1
  440.9 18.3 %shard_map.102 = (f32[784,4,800]{2,1,0:T(4,128)}, f32[784,4,800]{2,1,0:T(4,128)}) custom-call(f32[8,400,768]{2,1,0:T(8,128)} %get-tuple-element.11.gw, f32[8,24,400]{2,1,0:T(8,128)S(1)} %copy-done.1, f32[8,400,768]{2,1,0:T(8,128)} %get-tuple-element.13.gp, f32[8,24,400]{2,1,0:T(8,128)S(1)} %copy-done), custom_call_target="tpu_custom_call" | custom-call | tf_op jit(solution)/shard_map/pallas_call | solution.py:391
  459.2 0.1 slice_reduce_fusion
  459.3 0.7 reshape_squeeze.10
  460.0 0.7 reshape_squeeze.9
  460.7 0.9 slice_reduce_fusion.2
  461.6 0.1 reshape_squeeze.11
  461.7 0.6 reduce_sum.9
Async XLA Ops:
  438.9 1.0 copy-start
  439.9 1.0 copy-start.1

commit v3 on v2

--- a/solution.py
+++ b/solution.py
@@ -10,8 +10,8 @@
 LEAPS = 16
 PRIOR_VAR = 1.0
 MAIN = 768
-BLOCK = 2048
-CHUNK = 512
+BLOCK = 4096
+CHUNK = 256
 DEPTH = 512
 PIECE = 512
 SMALL = 24
@@ -21,15 +21,15 @@
 NT = (((1,), (1,)), ((), ()))
 
 
-def chain_kernel(step, x_hbm, xr_ref, lab_ref, w1_hbm, w2_ref, p1_hbm, p2_ref,
+def chain_kernel(step, x_hbm, lab_ref, w1_hbm, w2_ref, p1_hbm, p2_ref,
                  end_w, end_ws, end_p, end_ps,
-                 xm, xr, lab, stage, turn, act, bt, gm, gr, g2, wm, wr, v, pm, pr, q, wmb, wrb,
+                 xt, lab, stage, turn, act, bt, gm, g2, wm, v, pm, q, wmb,
                  z_own, z_peer, small_w, small_p,
                  load_sem, x_send, x_recv, send_sem, recv_sem, end_send, end_recv, end_load):
-    num_rows = xm.shape[0]
+    num_feat, num_rows = xt.shape
     num_block = num_rows // BLOCK
     half = wm.shape[0]
-    rest = xr.shape[0]
+    rest = num_feat - MAIN
     me = lax.axis_index("data")
     chip = me // 2
     core = lax.rem(me, 2)
@@ -50,14 +50,13 @@
     own = [2 * core, 2 * core + 1]
     mine = rows_of(core, 2 * PIECE)
     loads = [
-        pltpu.make_async_copy(x_hbm.at[:, pl.ds(0, MAIN)], xm.at[mine, :], load_sem.at[0]),
-        pltpu.make_async_copy(xr_ref, xr.at[:, mine], load_sem.at[1]),
-        pltpu.make_async_copy(lab_ref, lab.at[:, mine], load_sem.at[2]),
+        pltpu.make_async_copy(x_hbm, xt.at[:, mine], load_sem.at[0]),
+        pltpu.make_async_copy(lab_ref, lab.at[:, mine], load_sem.at[1]),
     ]
     for c in loads:
         c.start()
-    load_w = pltpu.make_async_copy(w1_hbm, stage, load_sem.at[3])
-    load_p = pltpu.make_async_copy(p1_hbm, stage, load_sem.at[4])
+    load_w = pltpu.make_async_copy(w1_hbm, stage, load_sem.at[2])
+    load_p = pltpu.make_async_copy(p1_hbm, stage, load_sem.at[3])
     load_w.start()
     pl.semaphore_wait(barrier, 3)
     for c in loads:
@@ -65,7 +64,7 @@
 
     def x_copies(src, dst, device, ticket):
         a, b = rows_of(src, PIECE), rows_of(dst, PIECE)
-        pairs = ((xm.at[a, :], xm.at[b, :]), (xr.at[:, a], xr.at[:, b]), (lab.at[:, a], lab.at[:, b]))
+        pairs = ((xt.at[:, a], xt.at[:, b]), (lab.at[:, a], lab.at[:, b]))
         return [pltpu.make_async_remote_copy(
             src_ref=s, dst_ref=d, send_sem=x_send.at[i, ticket], recv_sem=x_recv.at[i, dst],
             device_id={"data": device}, device_id_type=MESH) for i, (s, d) in enumerate(pairs)]
@@ -93,29 +92,28 @@
         x_go(own[h], near_pos(h, 1, core), y_near, 3 * h + 1)
         x_go(own[h], own[h], peer, 3 * h + 2)
 
-    def part_of(w, m, r, as_bf16):
+    def part_of(out):
         for d in range(MAIN // 128):
             turn[:, d * 128:(d + 1) * 128] = stage[d * 128:(d + 1) * 128, chip, :].T
-        span = pl.ds(pl.multiple_of(core * half, 8), half)
-        m[...] = turn[span, :]
         tail = stage[MAIN:MAIN + rest, chip, :]
         tail = jnp.concatenate([tail, jnp.zeros((128 - rest, tail.shape[1]), F32)], axis=0)
-        turn[:, 0:128] = tail.T
-        r[...] = turn[span, 0:rest]
+        turn[:, MAIN:MAIN + rest] = tail.T[:, 0:rest]
+        out[...] = turn[pl.ds(pl.multiple_of(core * half, 8), half), :]
 
     def row_of(u, out):
         turn[:, 0:128] = jnp.broadcast_to(u[pl.ds(chip, 1), :], (128, u.shape[1])).T
         out[...] = turn[pl.ds(pl.multiple_of(core * half, 8), half), 0:128]
 
     load_w.wait()
-    part_of(None, wm, wr, True)
+    part_of(wm)
     load_p.start()
     row_of(w2_ref, v)
     wmb[...] = wm[...].astype(BF16)
-    wrb[...] = wr[...].astype(BF16)
     row_of(p2_ref, q)
     load_p.wait()
-    part_of(None, pm, pr, False)
+    part_of(pm)
+    gm[...] = jnp.zeros_like(gm)
+    g2[...] = jnp.zeros_like(g2)
 
     other = 1 - core
     x_arrived(2 * other)
@@ -156,8 +154,8 @@
         base = block * BLOCK
         for n in range(BLOCK // CHUNK):
             rows = pl.ds(pl.multiple_of(base + n * CHUNK, CHUNK), CHUNK)
-            pre = lax.dot_general(wmb[...], xm[rows, :], NT, preferred_element_type=F32)
-            pre = pre + jnp.dot(wrb[...], xr[:, rows], preferred_element_type=F32)
+            pre = jnp.dot(wmb[:, 0:MAIN], xt[0:MAIN, rows], preferred_element_type=F32)
+            pre = pre + jnp.dot(wmb[:, MAIN:], xt[MAIN:, rows], preferred_element_type=F32)
             for j in range(CHUNK // 128):
                 cols = pl.ds(pl.multiple_of(base + n * CHUNK + j * 128, 128), 128)
                 t = jnp.tanh(pre[:, j * 128:(j + 1) * 128])
@@ -172,15 +170,14 @@
             for j in range(DEPTH // 128):
                 cols = pl.ds(pl.multiple_of(base + n * DEPTH + j * 128, 128), 128)
                 z = z_own[slot, :, cols] + z_peer[slot, :, cols]
-                r = lab[:, cols] - jax.nn.sigmoid(z)
+                r = lab[:, cols].astype(F32) - jax.nn.sigmoid(z)
                 t = act[:, cols]
                 rb = jnp.broadcast_to(r, t.shape)
                 bt[:, pl.ds(n * DEPTH + j * 128, 128)] = ((rb * v[...]) * (1.0 - t * t)).astype(BF16)
                 g2[...] += rb * t
             rows = pl.ds(pl.multiple_of(base + n * DEPTH, DEPTH), DEPTH)
             b = bt[:, n * DEPTH:(n + 1) * DEPTH]
-            gm[...] += jnp.dot(b, xm[rows, :], preferred_element_type=F32)
-            gr[...] += lax.dot_general(b, xr[:, rows], NT, preferred_element_type=F32)
+            gm[...] += lax.dot_general(b, xt[:, rows], NT, preferred_element_type=F32)
 
     big = (wm, pm)
     small = (small_w, small_p)
@@ -192,7 +189,7 @@
         if piece == 2:
             return small[t], out_small[t].at[source]
         span = pl.ds(piece * part, part)
-        return big[t].at[span, :], out_big[t].at[source, span, :]
+        return big[t].at[span, pl.ds(0, MAIN)], out_big[t].at[source, span, :]
 
     def end_copy(t, piece, source, device, ticket, first):
         src, dst = end_pair(t, piece, source)
@@ -236,8 +233,8 @@
             src, dst = end_pair(t, piece, me)
             pltpu.make_async_copy(src, dst, end_load.at[t, piece]).wait()
 
-    def pack_small(buf, r, u, extra):
-        wide = jnp.concatenate([r[...], u[:, 0:8], jnp.zeros((half, 104), F32)], axis=1)
+    def pack_small(buf, m, u, extra):
+        wide = jnp.concatenate([m[:, MAIN:MAIN + rest], u[:, 0:8], jnp.zeros((half, 104), F32)], axis=1)
         flat = wide.T
         buf[0:rest, :] = flat[0:rest, :]
         buf[rest:SMALL, :] = jnp.where(lax.broadcasted_iota(jnp.int32, (SMALL - rest, half), 0) == 0, flat[rest:SMALL, :], extra)
@@ -246,13 +243,9 @@
         slot = lax.rem(index, 2)
         edge = jnp.logical_or(index == 0, index == LEAPS)
         kick = jnp.where(edge, 0.5 * step, step).astype(F32)
-        gm[...] = jnp.zeros_like(gm)
-        gr[...] = jnp.zeros_like(gr)
-        g2[...] = jnp.zeros_like(g2)
-
         def stage_of(k, c):
-            for j in range(1, num_block):
-                @pl.when(jnp.logical_and(index == 0, k == j))
+            for j in range(1, 4):
+                @pl.when(jnp.logical_and(index == 0, k == j * 4 * PIECE // BLOCK))
                 def _():
                     arrivals(j)
 
@@ -267,23 +260,34 @@
 
         lax.fori_loop(0, num_block + 1, stage_of, 0)
 
-        pm[...] += kick * (gm[...] - wm[...] / PRIOR_VAR)
-        pr[...] += kick * (gr[...] - wr[...] / PRIOR_VAR)
-        q[...] += kick * (jnp.broadcast_to(jnp.sum(g2[...], axis=1, keepdims=True), g2.shape) - v[...] / PRIOR_VAR)
+        def update(moves):
+            for i in range(half // 16):
+                part = slice(16 * i, 16 * i + 16)
+                w, u = wm[part, :], v[part, :]
+                new = pm[part, :] + kick * (gm[part, :] - w / PRIOR_VAR)
+                pm[part, :] = new
+                total = jnp.broadcast_to(jnp.sum(g2[part, :], axis=1, keepdims=True), u.shape)
+                new_q = q[part, :] + kick * (total - u / PRIOR_VAR)
+                q[part, :] = new_q
+                if moves:
+                    w = w + step * new
+                    wm[part, :] = w
+                    wmb[part, :] = w.astype(BF16)
+                    v[part, :] = u + step * new_q
+                    gm[part, :] = jnp.zeros_like(w)
+                    g2[part, :] = jnp.zeros_like(u)
 
         @pl.when(index < LEAPS)
         def _():
-            new = wm[...] + step * pm[...]
-            wm[...] = new
-            wmb[...] = new.astype(BF16)
-            new = wr[...] + step * pr[...]
-            wr[...] = new
-            wrb[...] = new.astype(BF16)
-            v[...] += step * q[...]
+            update(True)
+
+        @pl.when(index == LEAPS)
+        def _():
+            update(False)
 
         @pl.when(index == LEAPS - 1)
         def _():
-            pack_small(small_w, wr, v, 0.0)
+            pack_small(small_w, wm, v, 0.0)
             end_begin(0)
         return carry
 
@@ -291,15 +295,15 @@
 
     last = LEAPS % 2
     z = z_own[last] + z_peer[last]
-    loss = jnp.maximum(z, 0.0) + jnp.log1p(jnp.exp(-jnp.abs(z))) - lab[...] * z
+    loss = jnp.maximum(z, 0.0) + jnp.log1p(jnp.exp(-jnp.abs(z))) - lab[...].astype(F32) * z
 
     def total(x):
         return jnp.sum(jnp.sum(x, axis=0, keepdims=True), axis=1, keepdims=True)
 
-    squares = total(wm[...] * wm[...]) + total(wr[...] * wr[...]) + total(v[...] * v[...]) / 128.0
-    moving = total(pm[...] * pm[...]) + total(pr[...] * pr[...]) + total(q[...] * q[...]) / 128.0
+    squares = total(wm[...] * wm[...]) + total(v[...] * v[...]) / 128.0
+    moving = total(pm[...] * pm[...]) + total(q[...] * q[...]) / 128.0
     energy = 0.5 * total(loss) + squares / (2.0 * PRIOR_VAR) + 0.5 * moving
-    pack_small(small_p, pr, q, energy)
+    pack_small(small_p, pm, q, energy)
     end_begin(1)
     end_relay(0)
     end_relay(1)
@@ -309,11 +313,10 @@
         x_sent(ticket)
 
 
-def run_kernel(step, xs, xr, lab, w1, w2, p1, p2, devices):
+def run_kernel(step, xs, lab, w1, w2, p1, p2, devices):
     num_feat, chains, hidden = w1.shape
-    num_rows = xs.shape[0] * devices
+    num_rows = xs.shape[1] * devices
     half = hidden // 2
-    rest = num_feat - MAIN
     vmem = pl.BlockSpec(memory_space=pltpu.VMEM)
     hbm = pl.BlockSpec(memory_space=pl.ANY)
     big = jax.ShapeDtypeStruct((devices, half, MAIN), F32)
@@ -323,34 +326,29 @@
     return pl.pallas_call(
         functools.partial(chain_kernel, step),
         out_shape=[big, small, big, small],
-        in_specs=[hbm, hbm, hbm, hbm, vmem, hbm, vmem],
+        in_specs=[hbm, hbm, hbm, vmem, hbm, vmem],
         out_specs=[hbm] * 4,
         scratch_shapes=[
-            pltpu.VMEM((num_rows, MAIN), BF16),
-            pltpu.VMEM((rest, num_rows), BF16),
-            pltpu.VMEM((1, num_rows), F32),
+            pltpu.VMEM((num_feat, num_rows), BF16),
+            pltpu.VMEM((1, num_rows), jnp.int32),
             pltpu.VMEM((num_feat, chains, hidden), F32),
-            pltpu.VMEM((hidden, MAIN), F32),
+            pltpu.VMEM((hidden, num_feat), F32),
             pltpu.VMEM((half, num_rows), F32),
             pltpu.VMEM((half, BLOCK), BF16),
-            pltpu.VMEM((half, MAIN), F32),
-            pltpu.VMEM((half, rest), F32),
+            pltpu.VMEM((half, num_feat), F32),
             pltpu.VMEM((half, 128), F32),
-            pltpu.VMEM((half, MAIN), F32),
-            pltpu.VMEM((half, rest), F32),
+            pltpu.VMEM((half, num_feat), F32),
             pltpu.VMEM((half, 128), F32),
-            pltpu.VMEM((half, MAIN), F32),
-            pltpu.VMEM((half, rest), F32),
+            pltpu.VMEM((half, num_feat), F32),
             pltpu.VMEM((half, 128), F32),
-            pltpu.VMEM((half, MAIN), BF16),
-            pltpu.VMEM((half, rest), BF16),
+            pltpu.VMEM((half, num_feat), BF16),
             pltpu.VMEM((2, 1, num_rows), F32),
             pltpu.VMEM((2, 1, num_rows), F32),
             pltpu.VMEM((SMALL, half), F32),
             pltpu.VMEM((SMALL, half), F32),
-            dma((5,)),
-            dma((3, 14)),
-            dma((3, 16)),
+            dma((4,)),
+            dma((2, 14)),
+            dma((2, 16)),
             dma((2, blocks)),
             dma((2, blocks)),
             dma((2, 3, 7)),
@@ -359,10 +357,10 @@
         ],
         compiler_params=pltpu.CompilerParams(
             collective_id=0, has_side_effects=True, vmem_limit_bytes=62 * 2 ** 20),
-    )(xs, xr, lab, w1, w2, p1, p2)
-
-
-def place_kernel(gw, gws, gp, gps, end_w, end_p):
+    )(xs, lab, w1, w2, p1, p2)
+
+
+def place_kernel(gw, gws, gp, gps, end_w, end_w2, end_p, end_p2, energy):
     step = pl.program_id(0)
     tiles = MAIN // 128
     chains = end_w.shape[1]
@@ -376,9 +374,15 @@
 
     @pl.when(step == tiles)
     def _():
-        for g, end in ((gws, end_w), (gps, end_p)):
+        for g, end, end2 in ((gws, end_w, end_w2), (gps, end_p, end_p2)):
             for c in range(chains):
-                end[0:rest, c, :] = jnp.concatenate([g[2 * c, 0:rest, :], g[2 * c + 1, 0:rest, :]], axis=1)
+                both = jnp.concatenate([g[2 * c], g[2 * c + 1]], axis=1)
+                end[0:rest, c, :] = both[0:rest, :]
+                end2[c:c + 1, :] = both[rest:rest + 1, :]
+        for c in range(chains):
+            row = slice(rest + 1, rest + 2)
+            sums = gps[2 * c, row, 0:128] + gps[2 * c + 1, row, 0:128]
+            energy[c:c + 1, :] = sums
 
 
 def place(gw, gws, gp, gps, num_feat, chains, hidden):
@@ -388,10 +392,14 @@
     small = pl.BlockSpec(gws.shape, lambda i: (0, 0, 0))
     out = pl.BlockSpec((128, chains, hidden), lambda i: (i, 0, 0))
     shape = jax.ShapeDtypeStruct((num_feat, chains, hidden), F32)
+    row = jax.ShapeDtypeStruct((chains, hidden), F32)
+    flat = pl.BlockSpec((chains, hidden), lambda i: (0, 0))
     return pl.pallas_call(
-        place_kernel, grid=(tiles + 1,), out_shape=[shape, shape],
-        in_specs=[big, small, big, small], out_specs=[out, out],
-        compiler_params=pltpu.CompilerParams(vmem_limit_bytes=48 * 2 ** 20),
+        place_kernel, grid=(tiles + 1,),
+        out_shape=[shape, row, shape, row, jax.ShapeDtypeStruct((chains, 128), F32)],
+        in_specs=[big, small, big, small],
+        out_specs=[out, flat, out, flat, pl.BlockSpec((chains, 128), lambda i: (0, 0))],
+        compiler_params=pltpu.CompilerParams(vmem_limit_bytes=62 * 2 ** 20),
     )(gw, gws, gp, gps)
 
 
@@ -409,15 +417,9 @@
         step = 1.0 / math.sqrt(num_rows * (num_feat + hidden))
 
         def device_body(x_rows, y_rows, w1, w2, p1, p2):
-            xr = x_rows[:, MAIN:].T
-            lab = y_rows.astype(F32)[None, :]
-            gw, gws, gp, gps = run_kernel(step, x_rows, xr, lab, w1, w2, p1, p2, devices)
-            end_w, end_p = place(gw, gws, gp, gps, num_feat, chains, hidden)
-            rest = num_feat - MAIN
-            end_w2 = gws[:, rest, :].reshape(chains, hidden)
-            end_p2 = gps[:, rest, :].reshape(chains, hidden)
-            energy = gps[:, rest + 1, 0].reshape(chains, 2).sum(axis=1)
-            return end_w, end_w2, end_p, end_p2, energy
+            gw, gws, gp, gps = run_kernel(step, x_rows.T, y_rows[None, :], w1, w2, p1, p2, devices)
+            *state, energy = place(gw, gws, gp, gps, num_feat, chains, hidden)
+            return *state, energy[:, 0]
 
         mapped = jax.shard_map(device_body, mesh=mesh, in_specs=(row_spec, label_spec, in_spec, out_spec, in_spec, out_spec), out_specs=(in_spec, out_spec, in_spec, out_spec, chain_spec), check_vma=False)
         return mapped(feats, labels, w_in, w_out, mom_in, mom_out)

time: 463 us -> 442 us (0.955)
  Pallas kernels: 450 us -> 439 us
  local copies, waits for them, and re-layouts: 9.49 us -> 1.3 us
    pallas_call x1, Pallas kernels: 432 us -> 421 us  [run_kernel(): pl.pallas_call(functools.partial(chain_kernel, step), out_shape=[big, sma...]
    unnamed x5 -> x0, local copies, waits for them, and re-layouts: 5.69 us -> none
where the time goes in v3:
time: 442 us; the launch traced here: 441 us
  Pallas kernels  439 us (99%)
    pallas_call x1, Pallas kernels, run_kernel(): pl.pallas_call(functools.partial(chain_kernel, step), out_shape=[big, sma...  421 us
    pallas_call x1, Pallas kernels, place(): pl.pallas_call(place_kernel, grid=(tiles + 1,), out_shape=[shape, row, sh...  18.7 us

profile of v3, /device:TPU:0, one launch (start us, length us, event | category | flops | bytes accessed | tf_op | source)
XLA Modules:
  0.0 441.2 jit_solution(335996538019747946)
XLA Ops:
  0.6 420.6 %shard_map.101 = (f32[8,400,768]{2,1,0:T(8,128)}, f32[8,24,400]{2,1,0:T(8,128)}, f32[8,400,768]{2,1,0:T(8,128)}, f32[8,24,400]{2,1,0:T(8,128)}) custom-call(bf16[784,1024]{1,0:T(8,128)(2,1)} %bitcast.2, s32[1,1024]{1,0:T(1,128)} %bitcast.3, f32[784,4,800]{2,1,0:T(4,128)} %w1_hbm.1, f32[4,800]{1,0:T(4,128)} %w2_ref.1, f32[784,4,800]{2,1,0:T(4,128)} %p1_hbm.1, ...), custom_call_target="tpu_custom_call" | custom-call | tf_op jit(solution)/shard_map/pallas_call | solution.py:326
  421.3 18.7 %shard_map.102 = (f32[784,4,800]{2,1,0:T(4,128)}, f32[4,800]{1,0:T(4,128)}, f32[784,4,800]{2,1,0:T(4,128)}, f32[4,800]{1,0:T(4,128)}, f32[4,128]{1,0:T(4,128)}) custom-call(f32[8,400,768]{2,1,0:T(8,128)} %get-tuple-element.14.gw, f32[8,24,400]{2,1,0:T(8,128)} %get-tuple-element.15.gws, f32[8,400,768]{2,1,0:T(8,128)} %get-tuple-element.16.gp, ...), custom_call_target="tpu_custom_call" | custom-call | tf_op jit(solution)/shard_map/pallas_call | solution.py:397
  439.9 1.3 slice_reduce_fusion

commit v4 on v3

--- a/solution.py
+++ b/solution.py
@@ -110,8 +110,6 @@
     row_of(w2_ref, v)
     wmb[...] = wm[...].astype(BF16)
     row_of(p2_ref, q)
-    load_p.wait()
-    part_of(pm)
     gm[...] = jnp.zeros_like(gm)
     g2[...] = jnp.zeros_like(g2)
 
@@ -248,6 +246,9 @@
                 @pl.when(jnp.logical_and(index == 0, k == j * 4 * PIECE // BLOCK))
                 def _():
                     arrivals(j)
+                    if j == 1:
+                        load_p.wait()
+                        part_of(pm)
 
             @pl.when(k < num_block)
             def _():

time: 442 us -> 441 us (level)
  no operation moved by 1% of the time
where the time goes in v4:
time: 441 us; the launch traced here: 440 us
  Pallas kernels  439 us (100%)
    pallas_call x1, Pallas kernels, run_kernel(): pl.pallas_call(functools.partial(chain_kernel, step), out_shape=[big, sma...  420 us
    pallas_call x1, Pallas kernels, place(): pl.pallas_call(place_kernel, grid=(tiles + 1,), out_shape=[shape, row, sh...  18.7 us

profile of v4, /device:TPU:0, one launch (start us, length us, event | category | flops | bytes accessed | tf_op | source)
XLA Modules:
  0.0 440.5 jit_solution(863360183637968629)
XLA Ops:
  0.6 419.8 %shard_map.101 = (f32[8,400,768]{2,1,0:T(8,128)}, f32[8,24,400]{2,1,0:T(8,128)}, f32[8,400,768]{2,1,0:T(8,128)}, f32[8,24,400]{2,1,0:T(8,128)}) custom-call(bf16[784,1024]{1,0:T(8,128)(2,1)} %bitcast.2, s32[1,1024]{1,0:T(1,128)} %bitcast.3, f32[784,4,800]{2,1,0:T(4,128)} %w1_hbm.1, f32[4,800]{1,0:T(4,128)} %w2_ref.1, f32[784,4,800]{2,1,0:T(4,128)} %p1_hbm.1, ...), custom_call_target="tpu_custom_call" | custom-call | tf_op jit(solution)/shard_map/pallas_call | solution.py:327
  420.5 18.7 %shard_map.102 = (f32[784,4,800]{2,1,0:T(4,128)}, f32[4,800]{1,0:T(4,128)}, f32[784,4,800]{2,1,0:T(4,128)}, f32[4,800]{1,0:T(4,128)}, f32[4,128]{1,0:T(4,128)}) custom-call(f32[8,400,768]{2,1,0:T(8,128)} %get-tuple-element.14.gw, f32[8,24,400]{2,1,0:T(8,128)} %get-tuple-element.15.gws, f32[8,400,768]{2,1,0:T(8,128)} %get-tuple-element.16.gp, ...), custom_call_target="tpu_custom_call" | custom-call | tf_op jit(solution)/shard_map/pallas_call | solution.py:398
  439.2 1.3 slice_reduce_fusion
